TPU v7x, 32 devices: a whole 2x2x4 slice. The times are simulated.
32 devices in a mesh: gx: 8 (over z, y), gy: 4 (over x, core).
Axes of the slice: x: 2, y: 2, z: 4, core: 2. Of those that a mesh axis runs over, the one named last changes fastest.
Arguments:
- electric: float32 [3, 128, 512, 128], P(None, 'gx', 'gy'), may hold values from -6 to 6
- magnetic: float32 [3, 128, 512, 128], P(None, 'gx', 'gy'), may hold values from -6 to 6
- retention: float32 [128, 512, 128], P('gx', 'gy'), may hold values from 0.5 to 1
- coupling: float32 [128, 512, 128], P('gx', 'gy'), may hold values from 0.1 to 0.5
- spectrum_real: float32 [4, 4, 128, 512], P(None, None, 'gx', 'gy'), may hold values from -6 to 6
- spectrum_imag: float32 [4, 4, 128, 512], P(None, None, 'gx', 'gy'), may hold values from -6 to 6
- phases: float32 [4], replicated, may hold values from -3.140625 to 3.140625
Outputs:
- next_electric: float32 [3, 128, 512, 128], P(None, 'gx', 'gy')
- next_magnetic: float32 [3, 128, 512, 128], P(None, 'gx', 'gy')
- next_real: float32 [4, 4, 128, 512], P(None, None, 'gx', 'gy')
- next_imag: float32 [4, 4, 128, 512], P(None, None, 'gx', 'gy')
- far_field: float32 [2, 4, 4, 256, 256], P(None, None, None, 'gx', 'gy')
All inputs are finite; a program needn't handle non-finite values.
Results may differ from a plain program's by a relative error of at most 0.000071.
Values sent between devices are 32-bit elements; how exact they have to be, the bound alone decides.
No kernel may reach another device: no remote copies, remote signals or barrier semaphores. Data moves between devices by JAX's collectives and lax.ppermute only.
A program may use at most 128 MiB of HBM per device.

v0:
```python
import math
import jax
import jax.numpy as jnp
from jax import lax
from jax.sharding import PartitionSpec as P

WAVES = 256
TOP_PLANE = 111
curl_step = 0.5


def passed_along(value, axis, by):
    devices = lax.axis_size(axis)
    pairs = [(i, i + by) for i in range(devices) if 0 <= i + by < devices]
    return lax.ppermute(value, axis, pairs)


def forward_diff(values, along):
    padded = jnp.pad(values, [(0, 1) if which == along else (0, 0) for which in range(values.ndim)])
    return lax.slice_in_dim(padded, 1, values.shape[along] + 1, axis=along) - values


def backward_diff(values, along):
    padded = jnp.pad(values, [(1, 0) if which == along else (0, 0) for which in range(values.ndim)])
    return values - lax.slice_in_dim(padded, 0, values.shape[along], axis=along)


def ahead_diff(values, border, along):
    upper = lax.slice_in_dim(values, 1, values.shape[along], axis=along)
    return jnp.concatenate([upper, border], axis=along) - values


def behind_diff(values, border, along):
    lower = lax.slice_in_dim(values, 0, values.shape[along] - 1, axis=along)
    return values - jnp.concatenate([border, lower], axis=along)


def tables(number, extent, offset):
    wave = 2 * jnp.arange(number, dtype=jnp.int32) + 1 - number
    places = offset + jnp.arange(extent, dtype=jnp.int32)
    folded = wave[:, None] * places[None, :] % (4 * number)
    angles = folded.astype(jnp.float32) * (math.pi / (2 * number))
    return (jnp.cos(angles), jnp.sin(angles))


def first_section(real_part, imag_part, cos_y, sin_y):
    highest = lax.Precision.HIGHEST
    part_real = jnp.einsum("cfxy,ky->cfxk", real_part, cos_y, precision=highest) + jnp.einsum(
        "cfxy,ky->cfxk", imag_part, sin_y, precision=highest
    )
    part_imag = jnp.einsum("cfxy,ky->cfxk", imag_part, cos_y, precision=highest) - jnp.einsum(
        "cfxy,ky->cfxk", real_part, sin_y, precision=highest
    )
    return (part_real, part_imag)


def second_section(part_real, part_imag, cos_x, sin_x):
    highest = lax.Precision.HIGHEST
    far_real = jnp.einsum("jx,cfxk->cfjk", cos_x, part_real, precision=highest) + jnp.einsum(
        "jx,cfxk->cfjk", sin_x, part_imag, precision=highest
    )
    far_imag = jnp.einsum("jx,cfxk->cfjk", cos_x, part_imag, precision=highest) - jnp.einsum(
        "jx,cfxk->cfjk", sin_x, part_real, precision=highest
    )
    return jnp.stack([far_real, far_imag])


def per_device(electric, magnetic, retention, coupling, spectrum_real, spectrum_imag, phases):
    elec_x, elec_y, elec_z = (electric[0], electric[1], electric[2])
    rows_elec = passed_along(electric[1:3, 0:1], "gx", -1)
    cols_elec = passed_along(electric[0:3:2, :, 0:1], "gy", -1)
    mag_x = magnetic[0] - curl_step * (
        ahead_diff(elec_z, cols_elec[1], 1) - forward_diff(elec_y, 2)
    )
    mag_y = magnetic[1] - curl_step * (
        forward_diff(elec_x, 2) - ahead_diff(elec_z, rows_elec[1], 0)
    )
    mag_z = magnetic[2] - curl_step * (
        ahead_diff(elec_y, rows_elec[0], 0) - ahead_diff(elec_x, cols_elec[0], 1)
    )
    next_magnetic = jnp.stack([mag_x, mag_y, mag_z])
    rows_magn = passed_along(next_magnetic[1:3, -1:], "gx", 1)
    cols_magn = passed_along(next_magnetic[0:3:2, :, -1:], "gy", 1)
    new_x = retention * elec_x + coupling * (
        behind_diff(mag_z, cols_magn[1], 1) - backward_diff(mag_y, 2)
    )
    new_y = retention * elec_y + coupling * (
        backward_diff(mag_x, 2) - behind_diff(mag_z, rows_magn[1], 0)
    )
    new_z = retention * elec_z + coupling * (
        behind_diff(mag_y, rows_magn[0], 0) - behind_diff(mag_x, cols_magn[0], 1)
    )
    next_electric = jnp.stack([new_x, new_y, new_z])
    tangent = jnp.stack(
        [
            new_x[:, :, TOP_PLANE],
            new_y[:, :, TOP_PLANE],
            mag_x[:, :, TOP_PLANE],
            mag_y[:, :, TOP_PLANE],
        ]
    )
    next_real = spectrum_real + tangent[:, None] * jnp.cos(phases)[None, :, None, None]
    next_imag = spectrum_imag - tangent[:, None] * jnp.sin(phases)[None, :, None, None]
    local_rows = electric.shape[1]
    local_cols = electric.shape[2]
    scale = 1.0 / math.sqrt(local_rows * lax.axis_size("gx") * local_cols * lax.axis_size("gy"))
    cos_y, sin_y = tables(WAVES, local_cols, lax.axis_index("gy") * local_cols)
    part_real, part_imag = first_section(next_real, next_imag, cos_y, sin_y)
    cos_full, sin_full = tables(WAVES, local_rows * lax.axis_size("gx"), 0)
    reduced = lax.psum_scatter(
        jnp.stack([part_real, part_imag]), "gy", scatter_dimension=4, tiled=True
    )
    columns = lax.all_to_all(reduced, "gx", split_axis=4, concat_axis=3, tiled=True)
    finished = second_section(columns[0], columns[1], cos_full, sin_full)
    whole = lax.all_to_all(finished, "gx", split_axis=3, concat_axis=4, tiled=True)
    far_field = whole * scale
    return (next_electric, next_magnetic, next_real, next_imag, far_field)


def solution(mesh):
    placed = (
        P(None, "gx", "gy", None),
        P(None, "gx", "gy", None),
        P("gx", "gy", None),
        P("gx", "gy", None),
        P(None, None, "gx", "gy"),
        P(None, None, "gx", "gy"),
        P(),
    )
    return jax.shard_map(
        per_device,
        mesh=mesh,
        in_specs=placed,
        out_specs=(
            P(None, "gx", "gy", None),
            P(None, "gx", "gy", None),
            P(None, None, "gx", "gy"),
            P(None, None, "gx", "gy"),
            P(None, None, None, "gx", "gy"),
        ),
        check_vma=False,
    )
```

profile of v0, /device:TPU:0, one launch (start us, length us, event | category | flops | bytes accessed | tf_op | source)
XLA Modules:
  0.0 151.3 jit_solution(2751149047137637543)
XLA Ops:
  8.1 1.3 collective-permute-start.1
  10.4 1.3 collective-permute-start
  11.7 2.3 %slice_bitcast_fusion.2 = f32[16,128,128]{2,1,0:T(8,128)} fusion(f32[3,16,128,128]{3,2,1,0:T(8,128)} %param.7), kind=kLoop, calls=%fused_computation.58 | loop fusion | bytes 2097152 | tf_op jit(solution)/shard_map/squeeze | solution.py:69
  14.0 3.4 %slice_bitcast_fusion.10 = (f32[15,128,128]{2,1,0:T(8,128)}, f32[1,15,128,128]{3,2,1,0:T(8,128)}, f32[15,128,128]{2,1,0:T(8,128)}) fusion(f32[3,16,128,128]{3,2,1,0:T(8,128)} %param.7), kind=kLoop, calls=%fused_computation.139 | loop fusion | bytes 4915200 | tf_op jit(solution)/shard_map/slice | solution.py:29
  17.5 2.8 %fusion.96 = (f32[16,127,128]{2,1,0:T(8,128)}, f32[1,16,127,128]{3,2,1,0:T(8,128)}) fusion(f32[16,128,128]{2,1,0:T(8,128)} %slice_bitcast_fusion.2), kind=kLoop, calls=%fused_computation.142 | loop fusion | bytes 3121152 | tf_op jit(solution)/shard_map/slice | solution.py:29
  20.4 2.5 %slice_bitcast_fusion = (f32[16,128,128]{2,1,0:T(8,128)S(1)}, f32[1,16,128,128]{3,2,1,0:T(8,128)S(1)}, f32[16,128,128]{2,1,0:T(8,128)S(1)}) fusion(f32[3,16,128,128]{3,2,1,0:T(8,128)S(1)} %copy-done, f32[1,16,1,128]{3,2,1,0:T(1,128)S(1)} %bitcast.155, f32[1,16,127,128]{3,2,1,0:T(8,128)} %get-tuple-element.55, f32[1,1,128,128]{3,2,1,0:T(8,128)S(1)} %get-tuple-element.60, ...), kind=kLoop, calls=%fused_computation.56 | loop fusion | flops 1835008 | bytes 9437184 | tf_op jit(solution)/shard_map/squeeze | solution.py:69
  24.3 1.8 %fusion.22 = (f32[16,128,128]{2,1,0:T(8,128)S(1)}, f32[16,128,128]{2,1,0:T(8,128)S(1)}, f32[16,128,128]{2,1,0:T(8,128)S(1)}) fusion(f32[1,128,128]{2,1,0:T(8,128)S(1)} %get-tuple-element.58, f32[15,128,128]{2,1,0:T(8,128)S(1)} %copy-done.9, f32[16,1,128]{2,1,0:T(1,128)S(1)} %bitcast.156, f32[16,127,128]{2,1,0:T(8,128)S(1)} %copy-done.7, ...), kind=kLoop, calls=%fused_computation.38 | loop fusion | flops 4980736 | bytes 15728640 | tf_op jit(solution)/shard_map/sub | solution.py:78
  26.1 1.2 slice_reduce_fusion
  27.6 3.3 %collective-permute-start.2 = (f32[2,16,1,128]{3,2,1,0:T(1,128)S(1)}, f32[2,16,1,128]{3,2,1,0:T(1,128)S(1)}, u32[]{:S(2)}, u32[]{:S(2)}) collective-permute-start(f32[2,16,1,128]{3,2,1,0:T(1,128)S(1)} %slice.139), channel_id=1, source_target_pairs={{0,1},{1,2},{2,3},{4,5},{5,6},{6,7},{8,9},{9,10},{10,11},{12,13},{... | collective-permute-start | bytes 49160 | tf_op jit(solution)/shard_map/ppermute | solution.py:15
  31.0 5.7 %collective-permute-start.3 = (f32[2,1,128,128]{3,2,1,0:T(8,128)S(1)}, f32[2,1,128,128]{3,2,1,0:T(8,128)S(1)}, u32[]{:S(2)}, u32[]{:S(2)}) collective-permute-start(f32[2,1,128,128]{3,2,1,0:T(8,128)S(1)} %pad_maximum_fusion.4), channel_id=1, source_target_pairs={{0,4},{4,8},{8,12},{12,16},{16,20},{20,24},{24,28},{1,5},{5,9},{9,... | collective-permute-start | bytes 393224 | tf_op jit(solution)/shard_map/ppermute | solution.py:15
  36.8 2.9 %collective-permute-done.3 = f32[2,1,128,128]{3,2,1,0:T(8,128)S(1)} collective-permute-done((f32[2,1,128,128]{3,2,1,0:T(8,128)S(1)}, f32[2,1,128,128]{3,2,1,0:T(8,128)S(1)}, u32[]{:S(2)}, u32[]{:S(2)}) %collective-permute-start.3) | collective-permute-done | bytes 131104 | tf_op jit(solution)/shard_map/ppermute | solution.py:15
  39.8 2.6 %fusion.15 = (f32[16,128,128]{2,1,0:T(8,128)S(1)}, f32[1,16,128,128]{3,2,1,0:T(8,128)}, f32[16,128,128]{2,1,0:T(8,128)S(1)}) fusion(f32[16,128,128]{2,1,0:T(8,128)S(1)} %copy-done.12, f32[16,128,128]{2,1,0:T(8,128)S(1)} %get-tuple-element.44, f32[16,128,128]{2,1,0:T(8,128)S(1)} %get-tuple-element.43, f32[16,127,128]{2,1,0:T(8,128)S(1)} %bitcast.149, ...), kind=kLoop, calls=%fused_computation.26 | loop fusion | flops 5767168 | bytes 15728640 | tf_op jit(solution)/shard_map/add | solution.py:84
  42.5 1.0 copy-done.2
  43.4 1.2 slice_reduce_fusion.2
  44.8 0.9 fusion.44
  46.6 0.9 fusion
  47.6 0.9 fusion.1
  48.6 3.4 %copy.200 = f32[2,4,4,16,256]{3,2,1,0,4:T(4,128)} copy(f32[2,4,4,16,256]{4,3,2,1,0:T(8,128)S(1)} %pad_maximum_fusion.2) | data formatting | bytes 1048576
  51.9 5.9 %reshape.43 = f32[256,512]{1,0:T(8,128)} reshape(f32[256,2,4,4,16]{4,3,2,1,0:T(4,128)} %bitcast.146) | data formatting | bytes 1048576
  57.9 24.4 %reduce-scatter.4.cloned.1.call-done = f32[64,512]{1,0:T(8,128)} async-done(((f32[256,512]{1,0:T(8,128)}), f32[64,512]{1,0:T(8,128)}) %reduce-scatter.4.cloned.1.call-update) | async-done | bytes 131088
  82.3 1.6 %reshape.44 = f32[64,2,4,4,16]{4,3,2,1,0:T(4,128)S(1)} reshape(f32[64,512]{1,0:T(8,128)} %reduce-scatter.4.cloned.1.call-done) | data formatting | bytes 262144
  84.8 12.7 %all_to_all.24 = f32[8,1,4096]{2,1,0:T(1,128)S(1)} all-to-all(f32[8,1,4096]{2,1,0:T(1,128)S(1)} %reshape.49), channel_id=1, replica_groups=mesh['gx'=8,'gy'=4] {'gx'}, dimensions={0} | all-to-all | bytes 262144 | tf_op jit(solution)/shard_map/all_to_all | solution.py:113
  104.3 3.3 %copy.193 = f32[2,4,4,256,8]{4,2,1,0,3:T(4,128)} copy(f32[2,4,4,256,8]{3,4,2,1,0:T(8,128)S(1)} %pad_maximum_fusion.3) | data formatting | bytes 524288 | tf_op jit(solution)/shard_map/stack | solution.py:65
  107.6 7.3 %reshape.51 = f32[8,1,8192]{2,1,0:T(1,128)} reshape(f32[256,2,4,4,8]{4,3,2,1,0:T(4,128)} %bitcast.148) | data formatting | bytes 524288
  114.9 3.7 %all-to-all-start.1 = ((f32[8,1,8192]{2,1,0:T(1,128)}), f32[8,1,8192]{2,1,0:T(1,128)S(1)}, u32[]{:S(2)}, u32[]{:S(2)}) async-start(f32[8,1,8192]{2,1,0:T(1,128)} %reshape.51), calls=%async_computation.1 | async-start | bytes 524288 | tf_op jit(solution)/shard_map/all_to_all | solution.py:115
  118.6 1.9 %pad_maximum_fusion.1 = f32[3,16,128,128]{3,2,1,0:T(8,128)} fusion(f32[1,16,128,128]{3,2,1,0:T(8,128)S(1)} %copy-done.8, f32[1,16,128,128]{3,2,1,0:T(8,128)S(1)} %bitcast.151, f32[1,16,128,128]{3,2,1,0:T(8,128)S(1)} %bitcast.150), kind=kLoop, calls=%fused_computation.1 | loop fusion | flops 1572864 | bytes 6291456 | tf_op jit(solution)/shard_map/stack | solution.py:93
  120.5 6.0 %all-to-all-done.1 = f32[8,1,8192]{2,1,0:T(1,128)S(1)} async-done(((f32[8,1,8192]{2,1,0:T(1,128)}), f32[8,1,8192]{2,1,0:T(1,128)S(1)}, u32[]{:S(2)}, u32[]{:S(2)}) %all-to-all-start.1) | async-done | bytes 262176 | tf_op jit(solution)/shard_map/all_to_all | solution.py:115
  126.5 1.2 reduce.9
  127.7 6.9 %reshape.52 = f32[256,2,4,4,8]{4,3,2,1,0:T(4,128)} reshape(f32[8,8192]{1,0:T(8,128)S(1)} %reduce.9) | data formatting | bytes 524288
  134.6 5.2 %broadcast_multiply_fusion = f32[2,4,4,256,8]{4,2,1,0,3:T(4,128)} fusion(f32[256,2,4,4,8]{4,3,2,1,0:T(4,128)} %reshape.52), kind=kLoop, calls=%fused_computation.2 | loop fusion | flops 65536 | bytes 524288 | tf_op jit(solution)/shard_map/mul | solution.py:116
  139.8 3.6 %copy.194 = f32[2,4,4,8,32,8]{4,5,3,2,1,0:T(8,128)S(1)} copy(f32[2,4,4,8,32,8]{5,2,1,0,4,3:T(4,128)} %bitcast.147) | data formatting | bytes 524288 | tf_op jit(solution)/shard_map/mul | solution.py:116
  143.4 1.1 copy.195
  (77 shorter events, 12.5 us)
Async XLA Ops:
  7.2 75.1 %reduce-scatter.4.cloned.1.call-start = ((), (), s32[]{:S(2)}) async-start(), calls=%async_computation.3 | async-start | bytes 655360
  8.1 12.2 %collective-permute-start.1 = (f32[2,16,1,128]{3,1,2,0:T(8,128)S(1)}, f32[2,16,1,128]{3,1,2,0:T(8,128)S(1)}, u32[]{:S(2)}, u32[]{:S(2)}) collective-permute-start(f32[2,16,1,128]{3,1,2,0:T(8,128)S(1)} %bitcast.162), channel_id=1, source_target_pairs={{1,0},{2,1},{3,2},{5,4},{6,5},{7,6},{9,8},{10,9},{11,10},{13,12},{... | collective-permute-start | bytes 49160 | tf_op jit(solution)/shard_map/ppermute | solution.py:15
  10.4 9.9 %collective-permute-start = (f32[2,1,128,128]{3,2,1,0:T(8,128)S(1)}, f32[2,1,128,128]{3,2,1,0:T(8,128)S(1)}, u32[]{:S(2)}, u32[]{:S(2)}) collective-permute-start(f32[2,1,128,128]{3,2,1,0:T(8,128)S(1)} %slice.123), channel_id=1, source_target_pairs={{4,0},{8,4},{12,8},{16,12},{20,16},{24,20},{28,24},{5,1},{9,5},{13... | collective-permute-start | bytes 393224 | tf_op jit(solution)/shard_map/ppermute | solution.py:15
  11.7 5.8 %copy-start.18 = (f32[4]{0:T(128)S(1)}, f32[4]{0:T(128)}, u32[]{:S(2)}) copy-start(f32[4]{0:T(128)} %param.13) | copy-start | bytes 52
  14.0 6.3 %copy-start = (f32[3,16,128,128]{3,2,1,0:T(8,128)S(1)}, f32[3,16,128,128]{3,2,1,0:T(8,128)}, u32[]{:S(2)}) copy-start(f32[3,16,128,128]{3,2,1,0:T(8,128)} %param.7) | copy-start | bytes 9437188
  20.3 2.7 %copy-start.1 = (f32[16,128,128]{2,1,0:T(8,128)S(1)}, f32[16,128,128]{2,1,0:T(8,128)}, u32[]{:S(2)}) copy-start(f32[16,128,128]{2,1,0:T(8,128)} %slice_bitcast_fusion.2) | copy-start | bytes 3145732
  20.4 3.1 %copy-start.6 = (f32[3,16,128,128]{3,2,1,0:T(8,128)S(1)}, f32[3,16,128,128]{3,2,1,0:T(8,128)}, u32[]{:S(2)}) copy-start(f32[3,16,128,128]{3,2,1,0:T(8,128)} %param.8) | copy-start | bytes 9437188
  20.4 3.4 %copy-start.7 = (f32[16,127,128]{2,1,0:T(8,128)S(1)}, f32[16,127,128]{2,1,0:T(8,128)}, u32[]{:S(2)}) copy-start(f32[16,127,128]{2,1,0:T(8,128)} %get-tuple-element.54) | copy-start | bytes 3121156
  20.4 3.7 %copy-start.9 = (f32[15,128,128]{2,1,0:T(8,128)S(1)}, f32[15,128,128]{2,1,0:T(8,128)}, u32[]{:S(2)}) copy-start(f32[15,128,128]{2,1,0:T(8,128)} %get-tuple-element.46) | copy-start | bytes 2949124
  20.4 4.0 %copy-start.10 = (f32[15,128,128]{2,1,0:T(8,128)S(1)}, f32[15,128,128]{2,1,0:T(8,128)}, u32[]{:S(2)}) copy-start(f32[15,128,128]{2,1,0:T(8,128)} %get-tuple-element.48) | copy-start | bytes 2949124
  27.5 12.3 %copy-start.11 = (f32[3,16,128,128]{3,2,1,0:T(8,128)}, f32[3,16,128,128]{3,2,1,0:T(8,128)S(1)}, u32[]{:S(2)}) copy-start(f32[3,16,128,128]{3,2,1,0:T(8,128)S(1)} %pad_maximum_fusion) | copy-start | bytes 9437188
  27.5 12.2 %copy-start.12 = (f32[16,128,128]{2,1,0:T(8,128)S(1)}, f32[16,128,128]{2,1,0:T(8,128)}, u32[]{:S(2)}) copy-start(f32[16,128,128]{2,1,0:T(8,128)} %param.10) | copy-start | bytes 3145732
  27.5 12.2 %copy-start.13 = (f32[16,128,128]{2,1,0:T(8,128)S(1)}, f32[16,128,128]{2,1,0:T(8,128)}, u32[]{:S(2)}) copy-start(f32[16,128,128]{2,1,0:T(8,128)} %param.9) | copy-start | bytes 3145732
  27.6 9.2 %collective-permute-start.2 = (f32[2,16,1,128]{3,2,1,0:T(1,128)S(1)}, f32[2,16,1,128]{3,2,1,0:T(1,128)S(1)}, u32[]{:S(2)}, u32[]{:S(2)}) collective-permute-start(f32[2,16,1,128]{3,2,1,0:T(1,128)S(1)} %slice.139), channel_id=1, source_target_pairs={{0,1},{1,2},{2,3},{4,5},{5,6},{6,7},{8,9},{9,10},{10,11},{12,13},{... | collective-permute-start | bytes 49160 | tf_op jit(solution)/shard_map/ppermute | solution.py:15
  31.0 8.8 %collective-permute-start.3 = (f32[2,1,128,128]{3,2,1,0:T(8,128)S(1)}, f32[2,1,128,128]{3,2,1,0:T(8,128)S(1)}, u32[]{:S(2)}, u32[]{:S(2)}) collective-permute-start(f32[2,1,128,128]{3,2,1,0:T(8,128)S(1)} %pad_maximum_fusion.4), channel_id=1, source_target_pairs={{0,4},{4,8},{8,12},{12,16},{16,20},{20,24},{24,28},{1,5},{5,9},{9,... | collective-permute-start | bytes 393224 | tf_op jit(solution)/shard_map/ppermute | solution.py:15
  39.8 4.8 %copy-start.16 = (f32[4,4,16,128]{3,2,1,0:T(8,128)S(1)}, f32[4,4,16,128]{3,2,1,0:T(8,128)}, u32[]{:S(2)}) copy-start(f32[4,4,16,128]{3,2,1,0:T(8,128)} %param.12) | copy-start | bytes 393220
  39.8 4.8 %copy-start.17 = (f32[4,4,16,128]{3,2,1,0:T(8,128)S(1)}, f32[4,4,16,128]{3,2,1,0:T(8,128)}, u32[]{:S(2)}) copy-start(f32[4,4,16,128]{3,2,1,0:T(8,128)} %param.11) | copy-start | bytes 393220
  42.5 1.0 copy-start.2
  42.5 2.2 %copy-start.4 = (f32[16,128,128]{2,1,0:T(8,128)}, f32[16,128,128]{2,1,0:T(8,128)S(1)}, u32[]{:S(2)}) copy-start(f32[16,128,128]{2,1,0:T(8,128)S(1)} %get-tuple-element.42) | copy-start | bytes 3145732
  44.8 2.8 %copy-start.15 = (f32[4,4,16,128]{3,2,1,0:T(8,128)}, f32[4,4,16,128]{3,2,1,0:T(8,128)S(1)}, u32[]{:S(2)}) copy-start(f32[4,4,16,128]{3,2,1,0:T(8,128)S(1)} %get-tuple-element.62) | copy-start | bytes 393220
  44.8 7.2 %copy-start.14 = (f32[4,4,16,128]{3,2,1,0:T(8,128)}, f32[4,4,16,128]{3,2,1,0:T(8,128)S(1)}, u32[]{:S(2)}) copy-start(f32[4,4,16,128]{3,2,1,0:T(8,128)S(1)} %get-tuple-element.61) | copy-start | bytes 393220
  107.6 11.0 %copy-start.3 = (f32[16,128,128]{2,1,0:T(8,128)S(1)}, f32[16,128,128]{2,1,0:T(8,128)}, u32[]{:S(2)}) copy-start(f32[16,128,128]{2,1,0:T(8,128)} %copy-done.2) | copy-start | bytes 3145732
  107.6 11.0 %copy-start.5 = (f32[16,128,128]{2,1,0:T(8,128)S(1)}, f32[16,128,128]{2,1,0:T(8,128)}, u32[]{:S(2)}) copy-start(f32[16,128,128]{2,1,0:T(8,128)} %copy-done.4) | copy-start | bytes 3145732
  107.6 11.0 %copy-start.8 = (f32[1,16,128,128]{3,2,1,0:T(8,128)S(1)}, f32[1,16,128,128]{3,2,1,0:T(8,128)}, u32[]{:S(2)}) copy-start(f32[1,16,128,128]{3,2,1,0:T(8,128)} %get-tuple-element.41) | copy-start | bytes 3145732
  114.9 11.6 %all-to-all-start.1 = ((f32[8,1,8192]{2,1,0:T(1,128)}), f32[8,1,8192]{2,1,0:T(1,128)S(1)}, u32[]{:S(2)}, u32[]{:S(2)}) async-start(f32[8,1,8192]{2,1,0:T(1,128)} %reshape.51), calls=%async_computation.1 | async-start | bytes 524288 | tf_op jit(solution)/shard_map/all_to_all | solution.py:115
Sparse Core Ops, SparseCore 0:
  58.0 24.2 reduce-scatter.3
where the time goes:
time: 152 us; the launch traced here: 151 us
  local copies, waits for them, and re-layouts  52 us (34%)
  waiting for transfers between devices  33.3 us (22%)
  other arithmetic  16.4 us (11%)
  starting transfers between devices  15.3 us (10%)
  between operations  14.6 us (10%)
  blocking collectives  12.7 us (8%)
  matrix products  6.97 us (5%)
    unnamed x47, local copies, waits for them, and re-layouts  30.3 us
    unnamed x2, waiting for transfers between devices  24.4 us
    all_to_all x1, blocking collectives, per_device(): lax.all_to_all(reduced, 'gx', split_axis=4, concat_axis=3, tiled=True)  12.7 us
    ppermute x4, starting transfers between devices, passed_along(): return lax.ppermute(value, axis, pairs)  11.6 us
    slice x3, local copies, waits for them, and re-layouts, ahead_diff(): upper = lax.slice_in_dim(values, 1, values.shape[along], axis=along)  6.34 us
    all_to_all x1, waiting for transfers between devices, per_device(): lax.all_to_all(finished, 'gx', split_axis=3, concat_axis=4, tiled=True)  6 us
    mul x1, other arithmetic, per_device(): far_field = whole * scale  5.21 us
    all_to_all x1, starting transfers between devices, per_device(): lax.all_to_all(finished, 'gx', split_axis=3, concat_axis=4, tiled=True)  3.67 us
  transfers between devices with their start and end apart: 6, of which 3 were waited for; matrix products, arithmetic and copies ran while one was open for 8% of the time, Pallas kernels for 0%

commit v1 on v0

--- a/solution.py
+++ b/solution.py
@@ -110,7 +110,10 @@
     reduced = lax.psum_scatter(
         jnp.stack([part_real, part_imag]), "gy", scatter_dimension=4, tiled=True
     )
-    columns = lax.all_to_all(reduced, "gx", split_axis=4, concat_axis=3, tiled=True)
+    columns = jnp.concatenate(
+        lax.all_to_all(jnp.stack(jnp.split(reduced, lax.axis_size("gx"), axis=4)), "gx", 0, 0),
+        axis=3,
+    )
     finished = second_section(columns[0], columns[1], cos_full, sin_full)
     whole = lax.all_to_all(finished, "gx", split_axis=3, concat_axis=4, tiled=True)
     far_field = whole * scale

time: 152 us -> 159 us (1.046)
  local copies, waits for them, and re-layouts: 52 us -> 58.3 us
    unnamed x47 -> x63, local copies, waits for them, and re-layouts: 30.3 us -> 38.5 us
    squeeze x1, local copies, waits for them, and re-layouts: 2.3 us -> 0.09 us  [per_device(): elec_x, elec_y, elec_z = (electric[0], electric[1], electric[2])]
  transfers between devices with their start and end apart: 6 -> 6, of which waited for: 3 -> 3; matrix products, arithmetic and copies ran while one was open for 8% -> 5% of each run, Pallas kernels for 0% -> 0%
where the time goes in v1:
time: 159 us
  local copies, waits for them, and re-layouts  58.3 us (37%)
  waiting for transfers between devices  33.9 us (21%)
  other arithmetic  16.7 us (11%)
  starting transfers between devices  15.3 us (10%)
  between operations  14.7 us (9%)
  blocking collectives  12.7 us (8%)
  matrix products  6.97 us (4%)
    unnamed x63, local copies, waits for them, and re-layouts  38.5 us
    unnamed x2, waiting for transfers between devices  24.9 us
    all_to_all x1, blocking collectives, per_device(): lax.all_to_all(jnp.stack(jnp.split(reduced, lax.axis_size('gx'), axis=4))...  12.7 us
    ppermute x4, starting transfers between devices, passed_along(): return lax.ppermute(value, axis, pairs)  11.6 us
    all_to_all x1, waiting for transfers between devices, per_device(): lax.all_to_all(finished, 'gx', split_axis=3, concat_axis=4, tiled=True)  6 us
    mul x1, other arithmetic, per_device(): far_field = whole * scale  5.2 us
    slice x3, local copies, waits for them, and re-layouts, ahead_diff(): upper = lax.slice_in_dim(values, 1, values.shape[along], axis=along)  4.97 us
    all_to_all x1, starting transfers between devices, per_device(): lax.all_to_all(finished, 'gx', split_axis=3, concat_axis=4, tiled=True)  3.67 us
  transfers between devices with their start and end apart: 6, of which 3 were waited for; matrix products, arithmetic and copies ran while one was open for 5% of the time, Pallas kernels for 0%

profile of v1, /device:TPU:0, one launch (start us, length us, event | category | flops | bytes accessed | tf_op | source)
XLA Modules:
  0.0 158.5 jit_solution(895731502851070218)
XLA Ops:
  7.2 1.1 slice.123
  8.3 1.3 collective-permute-start
  10.5 1.3 collective-permute-start.1
  11.8 3.3 %slice_bitcast_fusion.10 = (f32[15,128,128]{2,1,0:T(8,128)}, f32[1,15,128,128]{3,2,1,0:T(8,128)}, f32[15,128,128]{2,1,0:T(8,128)}) fusion(f32[3,16,128,128]{3,2,1,0:T(8,128)} %param.7), kind=kLoop, calls=%fused_computation.146 | loop fusion | bytes 4915200 | tf_op jit(solution)/shard_map/slice | solution.py:29
  16.2 1.6 fusion.97
  18.0 2.5 %slice_bitcast_fusion = (f32[16,128,128]{2,1,0:T(8,128)S(1)}, f32[1,16,128,128]{3,2,1,0:T(8,128)S(1)}, f32[16,128,128]{2,1,0:T(8,128)S(1)}) fusion(f32[3,16,128,128]{3,2,1,0:T(8,128)S(1)} %copy-done, f32[1,16,1,128]{3,2,1,0:T(1,128)S(1)} %bitcast.167, f32[1,16,127,128]{3,2,1,0:T(8,128)} %get-tuple-element.63, f32[1,1,128,128]{3,2,1,0:T(8,128)S(1)} %get-tuple-element.68, ...), kind=kLoop, calls=%fused_computation.55 | loop fusion | flops 1835008 | bytes 9437184 | tf_op jit(solution)/shard_map/squeeze | solution.py:69
  21.9 1.8 %fusion.22 = (f32[16,128,128]{2,1,0:T(8,128)S(1)}, f32[16,128,128]{2,1,0:T(8,128)S(1)}, f32[16,128,128]{2,1,0:T(8,128)S(1)}) fusion(f32[1,128,128]{2,1,0:T(8,128)S(1)} %get-tuple-element.66, f32[15,128,128]{2,1,0:T(8,128)S(1)} %copy-done.10, f32[16,1,128]{2,1,0:T(1,128)S(1)} %bitcast.168, f32[16,127,128]{2,1,0:T(8,128)S(1)} %copy-done.8, ...), kind=kLoop, calls=%fused_computation.38 | loop fusion | flops 4980736 | bytes 15728640 | tf_op jit(solution)/shard_map/sub | solution.py:78
  23.7 1.2 slice_reduce_fusion
  25.1 3.3 %collective-permute-start.2 = (f32[2,16,1,128]{3,2,1,0:T(1,128)S(1)}, f32[2,16,1,128]{3,2,1,0:T(1,128)S(1)}, u32[]{:S(2)}, u32[]{:S(2)}) collective-permute-start(f32[2,16,1,128]{3,2,1,0:T(1,128)S(1)} %slice.139), channel_id=1, source_target_pairs={{0,1},{1,2},{2,3},{4,5},{5,6},{6,7},{8,9},{9,10},{10,11},{12,13},{... | collective-permute-start | bytes 49160 | tf_op jit(solution)/shard_map/ppermute | solution.py:15
  28.5 5.7 %collective-permute-start.3 = (f32[2,1,128,128]{3,2,1,0:T(8,128)S(1)}, f32[2,1,128,128]{3,2,1,0:T(8,128)S(1)}, u32[]{:S(2)}, u32[]{:S(2)}) collective-permute-start(f32[2,1,128,128]{3,2,1,0:T(8,128)S(1)} %pad_maximum_fusion.4), channel_id=1, source_target_pairs={{0,4},{4,8},{8,12},{12,16},{16,20},{20,24},{24,28},{1,5},{5,9},{9,... | collective-permute-start | bytes 393224 | tf_op jit(solution)/shard_map/ppermute | solution.py:15
  34.4 2.9 %collective-permute-done.3 = f32[2,1,128,128]{3,2,1,0:T(8,128)S(1)} collective-permute-done((f32[2,1,128,128]{3,2,1,0:T(8,128)S(1)}, f32[2,1,128,128]{3,2,1,0:T(8,128)S(1)}, u32[]{:S(2)}, u32[]{:S(2)}) %collective-permute-start.3) | collective-permute-done | bytes 131104 | tf_op jit(solution)/shard_map/ppermute | solution.py:15
  37.4 2.6 %fusion.15 = (f32[16,128,128]{2,1,0:T(8,128)S(1)}, f32[1,16,128,128]{3,2,1,0:T(8,128)}, f32[16,128,128]{2,1,0:T(8,128)S(1)}) fusion(f32[16,128,128]{2,1,0:T(8,128)S(1)} %copy-done.13, f32[16,128,128]{2,1,0:T(8,128)S(1)} %get-tuple-element.44, f32[16,128,128]{2,1,0:T(8,128)S(1)} %get-tuple-element.43, f32[16,127,128]{2,1,0:T(8,128)S(1)} %bitcast.161, ...), kind=kLoop, calls=%fused_computation.26 | loop fusion | flops 5767168 | bytes 15728640 | tf_op jit(solution)/shard_map/add | solution.py:84
  41.0 1.2 slice_reduce_fusion.2
  46.1 3.4 %copy.192 = f32[2,4,4,16,256]{3,2,1,0,4:T(4,128)} copy(f32[2,4,4,16,256]{4,3,2,1,0:T(8,128)S(1)} %pad_maximum_fusion.2) | data formatting | bytes 1048576
  49.5 5.9 %reshape.48 = f32[256,512]{1,0:T(8,128)} reshape(f32[256,2,4,4,16]{4,3,2,1,0:T(4,128)} %bitcast.158) | data formatting | bytes 1048576
  55.5 24.9 %reduce-scatter.4.cloned.1.call-done = f32[64,512]{1,0:T(8,128)} async-done(((f32[256,512]{1,0:T(8,128)}), f32[64,512]{1,0:T(8,128)}) %reduce-scatter.4.cloned.1.call-update) | async-done | bytes 131088
  80.4 1.6 %reshape.49 = f32[64,2,4,4,16]{4,3,2,1,0:T(4,128)S(1)} reshape(f32[64,512]{1,0:T(8,128)} %reduce-scatter.4.cloned.1.call-done) | data formatting | bytes 262144
  84.7 1.0 copy.198
  85.8 1.0 copy.199
  86.8 1.0 copy.200
  87.9 1.0 copy.201
  92.2 12.7 %all_to_all.14 = f32[8,1,4096]{2,1,0:T(1,128)S(1)} all-to-all(f32[8,1,4096]{2,1,0:T(1,128)S(1)} %reshape.54), channel_id=1, replica_groups=mesh['gx'=8,'gy'=4] {'gx'}, dimensions={0} | all-to-all | bytes 262144 | tf_op jit(solution)/shard_map/all_to_all | solution.py:114
  111.3 3.3 %copy.185 = f32[2,4,4,256,8]{4,2,1,0,3:T(4,128)} copy(f32[2,4,4,256,8]{3,4,2,1,0:T(8,128)S(1)} %pad_maximum_fusion.3) | data formatting | bytes 524288 | tf_op jit(solution)/shard_map/stack | solution.py:65
  114.7 7.3 %reshape.56 = f32[8,1,8192]{2,1,0:T(1,128)} reshape(f32[256,2,4,4,8]{4,3,2,1,0:T(4,128)} %bitcast.160) | data formatting | bytes 524288
  122.0 3.7 %all-to-all-start.1 = ((f32[8,1,8192]{2,1,0:T(1,128)}), f32[8,1,8192]{2,1,0:T(1,128)S(1)}, u32[]{:S(2)}, u32[]{:S(2)}) async-start(f32[8,1,8192]{2,1,0:T(1,128)} %reshape.56), calls=%async_computation.1 | async-start | bytes 524288 | tf_op jit(solution)/shard_map/all_to_all | solution.py:118
  125.7 1.9 %pad_maximum_fusion.1 = f32[3,16,128,128]{3,2,1,0:T(8,128)} fusion(f32[1,16,128,128]{3,2,1,0:T(8,128)S(1)} %copy-done.9, f32[1,16,128,128]{3,2,1,0:T(8,128)S(1)} %bitcast.163, f32[1,16,128,128]{3,2,1,0:T(8,128)S(1)} %bitcast.162), kind=kLoop, calls=%fused_computation.1 | loop fusion | flops 1572864 | bytes 6291456 | tf_op jit(solution)/shard_map/stack | solution.py:93
  127.6 6.0 %all-to-all-done.1 = f32[8,1,8192]{2,1,0:T(1,128)S(1)} async-done(((f32[8,1,8192]{2,1,0:T(1,128)}), f32[8,1,8192]{2,1,0:T(1,128)S(1)}, u32[]{:S(2)}, u32[]{:S(2)}) %all-to-all-start.1) | async-done | bytes 262176 | tf_op jit(solution)/shard_map/all_to_all | solution.py:118
  133.6 1.3 reduce.9
  134.9 6.9 %reshape.57 = f32[256,2,4,4,8]{4,3,2,1,0:T(4,128)} reshape(f32[8,8192]{1,0:T(8,128)S(1)} %reduce.9) | data formatting | bytes 524288
  141.8 5.2 %broadcast_multiply_fusion = f32[2,4,4,256,8]{4,2,1,0,3:T(4,128)} fusion(f32[256,2,4,4,8]{4,3,2,1,0:T(4,128)} %reshape.57), kind=kLoop, calls=%fused_computation.2 | loop fusion | flops 65536 | bytes 524288 | tf_op jit(solution)/shard_map/mul | solution.py:119
  147.0 3.6 %copy.186 = f32[2,4,4,8,32,8]{4,5,3,2,1,0:T(8,128)S(1)} copy(f32[2,4,4,8,32,8]{5,2,1,0,4,3:T(4,128)} %bitcast.159) | data formatting | bytes 524288 | tf_op jit(solution)/shard_map/mul | solution.py:119
  150.6 1.1 copy.187
  (96 shorter events, 21.1 us)
Async XLA Ops:
  7.2 8.0 %copy-start = (f32[3,16,128,128]{3,2,1,0:T(8,128)S(1)}, f32[3,16,128,128]{3,2,1,0:T(8,128)}, u32[]{:S(2)}) copy-start(f32[3,16,128,128]{3,2,1,0:T(8,128)} %param.7) | copy-start | bytes 9437188
  7.2 73.2 %reduce-scatter.4.cloned.1.call-start = ((), (), s32[]{:S(2)}) async-start(), calls=%async_computation.3 | async-start | bytes 655360
  8.3 9.6 %collective-permute-start = (f32[2,1,128,128]{3,2,1,0:T(8,128)S(1)}, f32[2,1,128,128]{3,2,1,0:T(8,128)S(1)}, u32[]{:S(2)}, u32[]{:S(2)}) collective-permute-start(f32[2,1,128,128]{3,2,1,0:T(8,128)S(1)} %slice.123), channel_id=1, source_target_pairs={{4,0},{8,4},{12,8},{16,12},{20,16},{24,20},{28,24},{5,1},{9,5},{13... | collective-permute-start | bytes 393224 | tf_op jit(solution)/shard_map/ppermute | solution.py:15
  10.5 7.3 %collective-permute-start.1 = (f32[2,16,1,128]{3,1,2,0:T(8,128)S(1)}, f32[2,16,1,128]{3,1,2,0:T(8,128)S(1)}, u32[]{:S(2)}, u32[]{:S(2)}) collective-permute-start(f32[2,16,1,128]{3,1,2,0:T(8,128)S(1)} %bitcast.174), channel_id=1, source_target_pairs={{1,0},{2,1},{3,2},{5,4},{6,5},{7,6},{9,8},{10,9},{11,10},{13,12},{... | collective-permute-start | bytes 49160 | tf_op jit(solution)/shard_map/ppermute | solution.py:15
  15.1 2.7 %copy-start.19 = (f32[4]{0:T(128)S(1)}, f32[4]{0:T(128)}, u32[]{:S(2)}) copy-start(f32[4]{0:T(128)} %param.13) | copy-start | bytes 52
  15.2 1.0 copy-start.1
  17.9 2.7 %copy-start.2 = (f32[16,128,128]{2,1,0:T(8,128)S(1)}, f32[16,128,128]{2,1,0:T(8,128)}, u32[]{:S(2)}) copy-start(f32[16,128,128]{2,1,0:T(8,128)} %copy-done.1) | copy-start | bytes 3145732
  17.9 3.1 %copy-start.7 = (f32[3,16,128,128]{3,2,1,0:T(8,128)S(1)}, f32[3,16,128,128]{3,2,1,0:T(8,128)}, u32[]{:S(2)}) copy-start(f32[3,16,128,128]{3,2,1,0:T(8,128)} %param.8) | copy-start | bytes 9437188
  17.9 3.4 %copy-start.8 = (f32[16,127,128]{2,1,0:T(8,128)S(1)}, f32[16,127,128]{2,1,0:T(8,128)}, u32[]{:S(2)}) copy-start(f32[16,127,128]{2,1,0:T(8,128)} %get-tuple-element.62) | copy-start | bytes 3121156
  17.9 3.7 %copy-start.10 = (f32[15,128,128]{2,1,0:T(8,128)S(1)}, f32[15,128,128]{2,1,0:T(8,128)}, u32[]{:S(2)}) copy-start(f32[15,128,128]{2,1,0:T(8,128)} %get-tuple-element.46) | copy-start | bytes 2949124
  18.0 4.0 %copy-start.11 = (f32[15,128,128]{2,1,0:T(8,128)S(1)}, f32[15,128,128]{2,1,0:T(8,128)}, u32[]{:S(2)}) copy-start(f32[15,128,128]{2,1,0:T(8,128)} %get-tuple-element.48) | copy-start | bytes 2949124
  25.1 12.3 %copy-start.12 = (f32[3,16,128,128]{3,2,1,0:T(8,128)}, f32[3,16,128,128]{3,2,1,0:T(8,128)S(1)}, u32[]{:S(2)}) copy-start(f32[3,16,128,128]{3,2,1,0:T(8,128)S(1)} %pad_maximum_fusion) | copy-start | bytes 9437188
  25.1 12.2 %copy-start.13 = (f32[16,128,128]{2,1,0:T(8,128)S(1)}, f32[16,128,128]{2,1,0:T(8,128)}, u32[]{:S(2)}) copy-start(f32[16,128,128]{2,1,0:T(8,128)} %param.10) | copy-start | bytes 3145732
  25.1 12.2 %copy-start.14 = (f32[16,128,128]{2,1,0:T(8,128)S(1)}, f32[16,128,128]{2,1,0:T(8,128)}, u32[]{:S(2)}) copy-start(f32[16,128,128]{2,1,0:T(8,128)} %param.9) | copy-start | bytes 3145732
  25.1 9.2 %collective-permute-start.2 = (f32[2,16,1,128]{3,2,1,0:T(1,128)S(1)}, f32[2,16,1,128]{3,2,1,0:T(1,128)S(1)}, u32[]{:S(2)}, u32[]{:S(2)}) collective-permute-start(f32[2,16,1,128]{3,2,1,0:T(1,128)S(1)} %slice.139), channel_id=1, source_target_pairs={{0,1},{1,2},{2,3},{4,5},{5,6},{6,7},{8,9},{9,10},{10,11},{12,13},{... | collective-permute-start | bytes 49160 | tf_op jit(solution)/shard_map/ppermute | solution.py:15
  28.5 8.8 %collective-permute-start.3 = (f32[2,1,128,128]{3,2,1,0:T(8,128)S(1)}, f32[2,1,128,128]{3,2,1,0:T(8,128)S(1)}, u32[]{:S(2)}, u32[]{:S(2)}) collective-permute-start(f32[2,1,128,128]{3,2,1,0:T(8,128)S(1)} %pad_maximum_fusion.4), channel_id=1, source_target_pairs={{0,4},{4,8},{8,12},{12,16},{16,20},{20,24},{24,28},{1,5},{5,9},{9,... | collective-permute-start | bytes 393224 | tf_op jit(solution)/shard_map/ppermute | solution.py:15
  37.4 4.8 %copy-start.17 = (f32[4,4,16,128]{3,2,1,0:T(8,128)S(1)}, f32[4,4,16,128]{3,2,1,0:T(8,128)}, u32[]{:S(2)}) copy-start(f32[4,4,16,128]{3,2,1,0:T(8,128)} %param.12) | copy-start | bytes 393220
  37.4 4.8 %copy-start.18 = (f32[4,4,16,128]{3,2,1,0:T(8,128)S(1)}, f32[4,4,16,128]{3,2,1,0:T(8,128)}, u32[]{:S(2)}) copy-start(f32[4,4,16,128]{3,2,1,0:T(8,128)} %param.11) | copy-start | bytes 393220
  40.0 1.0 copy-start.3
  40.0 2.2 %copy-start.5 = (f32[16,128,128]{2,1,0:T(8,128)}, f32[16,128,128]{2,1,0:T(8,128)S(1)}, u32[]{:S(2)}) copy-start(f32[16,128,128]{2,1,0:T(8,128)S(1)} %get-tuple-element.42) | copy-start | bytes 3145732
  42.3 2.8 %copy-start.15 = (f32[4,4,16,128]{3,2,1,0:T(8,128)}, f32[4,4,16,128]{3,2,1,0:T(8,128)S(1)}, u32[]{:S(2)}) copy-start(f32[4,4,16,128]{3,2,1,0:T(8,128)S(1)} %get-tuple-element.69) | copy-start | bytes 393220
  42.3 2.8 %copy-start.16 = (f32[4,4,16,128]{3,2,1,0:T(8,128)}, f32[4,4,16,128]{3,2,1,0:T(8,128)S(1)}, u32[]{:S(2)}) copy-start(f32[4,4,16,128]{3,2,1,0:T(8,128)S(1)} %get-tuple-element.70) | copy-start | bytes 393220
  114.7 11.0 %copy-start.4 = (f32[16,128,128]{2,1,0:T(8,128)S(1)}, f32[16,128,128]{2,1,0:T(8,128)}, u32[]{:S(2)}) copy-start(f32[16,128,128]{2,1,0:T(8,128)} %copy-done.3) | copy-start | bytes 3145732
  114.7 11.0 %copy-start.6 = (f32[16,128,128]{2,1,0:T(8,128)S(1)}, f32[16,128,128]{2,1,0:T(8,128)}, u32[]{:S(2)}) copy-start(f32[16,128,128]{2,1,0:T(8,128)} %copy-done.5) | copy-start | bytes 3145732
  114.7 11.0 %copy-start.9 = (f32[1,16,128,128]{3,2,1,0:T(8,128)S(1)}, f32[1,16,128,128]{3,2,1,0:T(8,128)}, u32[]{:S(2)}) copy-start(f32[1,16,128,128]{3,2,1,0:T(8,128)} %get-tuple-element.41) | copy-start | bytes 3145732
  122.0 11.6 %all-to-all-start.1 = ((f32[8,1,8192]{2,1,0:T(1,128)}), f32[8,1,8192]{2,1,0:T(1,128)S(1)}, u32[]{:S(2)}, u32[]{:S(2)}) async-start(f32[8,1,8192]{2,1,0:T(1,128)} %reshape.56), calls=%async_computation.1 | async-start | bytes 524288 | tf_op jit(solution)/shard_map/all_to_all | solution.py:118
Sparse Core Ops, SparseCore 0:
  55.6 24.7 reduce-scatter.3
